TPU v7x, 32 devices: a whole 2x2x4 slice. The times are simulated.
32 devices in a mesh: member: 2 (over y), lat: 4 (over z), lon: 4 (over x, core).
Axes of the slice: x: 2, y: 2, z: 4, core: 2. Of those that a mesh axis runs over, the one named last changes fastest.
Arguments:
- layer_inputs: bfloat16 [2, 256, 192, 512], P('member', None, 'lat', 'lon'), may hold values from -6 to 6
- conv_weight: bfloat16 [3, 3, 69, 256], replicated, may hold values from -0.125 to 0.125
- channel_offset: float32 [69], replicated, may hold values from -4 to 4
- observed: bfloat16 [69, 192, 512], P(None, 'lat', 'lon'), may hold values from -6 to 6
- var_weight: float32 [69], replicated, may hold values from 0.5 to 4
Outputs:
- predicted_fields: bfloat16 [2, 69, 192, 512], P('member', None, 'lat', 'lon')
- input_slope_field: bfloat16 [2, 256, 192, 512], P('member', None, 'lat', 'lon')
All inputs are finite; a program needn't handle non-finite values.
Results may differ from a plain program's by a relative error of at most 0.0063.
Values may be sent and summed in bfloat16 or wider, within the bound.
A program may use at most 192 MiB of HBM per device.

v0:
```python
import jax
import jax.numpy as jnp
from jax import lax
from jax.sharding import PartitionSpec as P

smoothing = 0.25


def extended(shard, sides, width, wrap):
    for axis, dim in sides:
        size, length = (lax.axis_size(axis), shard.shape[dim])
        up = [(i, (i + 1) % size) for i in range(size if wrap else size - 1)]
        down = [(j, i) for i, j in up]
        last = lax.slice_in_dim(shard, length - width, length, axis=dim)
        initial = lax.slice_in_dim(shard, 0, width, axis=dim)
        before = lax.ppermute(last, axis, up)
        after = lax.ppermute(initial, axis, down)
        shard = jnp.concatenate([before, shard, after], axis=dim)
    return shard


def smooth(difference):
    return difference * lax.rsqrt(difference * difference + smoothing * smoothing)


def extend(field):
    widened = extended(field, (("lon", 3),), 1, True)
    return extended(widened, (("lat", 2),), 1, False)


def pair_total(quantity_table, others):

    def add_member(member_index, running):
        member_values = lax.dynamic_index_in_dim(others, member_index, 0, keepdims=True).astype(
            jnp.float32
        )
        return running + smooth(quantity_table - member_values)

    return lax.fori_loop(
        0,
        others.shape[0],
        add_member,
        jnp.zeros(
            quantity_table.shape[:0] + (others.shape[0],) + quantity_table.shape[1:], jnp.float32
        ),
    )


def latitude_weight(first_row, count, total_rows):
    row_index = (first_row + jnp.arange(count)).astype(jnp.float32)
    return jnp.cos((-80.0 + 160.0 * (row_index + 0.5) / float(total_rows)) * (jnp.pi / 180.0))


def shards(layer_inputs, conv_weight, channel_offset, observed, var_weight):
    tile_rows = layer_inputs.shape[2]
    tile_cols = layer_inputs.shape[3]
    channels = layer_inputs.shape[1]
    outputs = conv_weight.shape[2]
    members = lax.axis_size("member")
    total_rows = tile_rows * lax.axis_size("lat")
    padded = extend(layer_inputs)[0]
    accumulated_outcome = jnp.zeros((outputs, tile_rows, tile_cols), jnp.float32)
    for row_tap in range(3):
        for col_tap in range(3):
            window = padded[:, row_tap : row_tap + tile_rows, col_tap : col_tap + tile_cols]
            accumulated_outcome = accumulated_outcome + lax.dot_general(
                conv_weight[row_tap, col_tap],
                window,
                (((1,), (0,)), ((), ())),
                preferred_element_type=jnp.float32,
            )
    predicted_fields = (accumulated_outcome + channel_offset[:, None, None]).astype(jnp.bfloat16)[
        None
    ]
    shard_realization_outputs = predicted_fields.astype(jnp.float32)
    received = lax.all_to_all(predicted_fields, "member", split_axis=2, concat_axis=0, tiled=True)
    pair_block = pair_total(received.astype(jnp.float32), received)
    pair_sums = lax.all_to_all(pair_block, "member", split_axis=0, concat_axis=2, tiled=True)
    lat_weight = latitude_weight(lax.axis_index("lat") * tile_rows, tile_rows, total_rows)
    target = observed.astype(jnp.float32)[None]
    gradient = (
        lat_weight[:, None]
        * var_weight[:, None, None]
        * (smooth(shard_realization_outputs - target) - pair_sums / (members - 1))
    ).astype(jnp.bfloat16)
    grad_padded = extend(gradient)[0]
    reverse_aggregate = jnp.zeros((channels, tile_rows, tile_cols), jnp.float32)
    for row_tap in range(3):
        for col_tap in range(3):
            window = grad_padded[
                :, 2 - row_tap : 2 - row_tap + tile_rows, 2 - col_tap : 2 - col_tap + tile_cols
            ]
            reverse_aggregate = reverse_aggregate + lax.dot_general(
                conv_weight[row_tap, col_tap],
                window,
                (((0,), (0,)), ((), ())),
                preferred_element_type=jnp.float32,
            )
    return (predicted_fields, reverse_aggregate.astype(jnp.bfloat16)[None])


def solution(mesh):
    in_specs = (P("member", None, "lat", "lon"), P(), P(), P(None, "lat", "lon"), P())
    out_specs = (P("member", None, "lat", "lon"), P("member", None, "lat", "lon"))
    return jax.shard_map(shards, mesh=mesh, in_specs=in_specs, out_specs=out_specs, check_vma=False)
```

profile of v0, /device:TPU:0, one launch (start us, length us, event | category | flops | bytes accessed | tf_op | source)
XLA Modules:
  0.0 176.8 jit_solution(11422943709343338945)
XLA Ops:
  0.6 6.9 %fusion.79 = (bf16[1,256,48,1]{3,2,1,0:T(8,128)(2,1)}, bf16[1,256,48,1]{3,2,1,0:T(8,128)(2,1)}) fusion(bf16[1,256,48,128]{3,2,1,0:T(8,128)(2,1)} %param.7), kind=kLoop, calls=%fused_computation.91 | loop fusion | bytes 98304 | tf_op jit(solution)/shard_map/slice | solution.py:14
  7.5 4.7 %copy.30 = bf16[1,256,48,1]{1,2,3,0:T(8,128)(2,1)S(1)} copy(bf16[1,256,48,1]{3,2,1,0:T(8,128)(2,1)} %get-tuple-element.113) | data formatting | bytes 49152
  12.2 0.5 collective-permute-start
  12.8 4.5 %copy.31 = bf16[1,256,48,1]{1,2,3,0:T(8,128)(2,1)S(1)} copy(bf16[1,256,48,1]{3,2,1,0:T(8,128)(2,1)} %get-tuple-element.114) | data formatting | bytes 49152
  17.3 2.0 %collective-permute-start.1 = (bf16[1,256,48,1]{1,2,3,0:T(8,128)(2,1)S(1)}, bf16[1,256,48,1]{1,2,3,0:T(8,128)(2,1)S(1)}, u32[]{:S(2)}, u32[]{:S(2)}) collective-permute-start(bf16[1,256,48,1]{1,2,3,0:T(8,128)(2,1)S(1)} %copy.31), channel_id=1, source_target_pairs={{1,0},{2,1},{3,2},{0,3},{5,4},{6,5},{7,6},{4,7},{9,8},{10,9},{11,1... | collective-permute-start | bytes 73736 | tf_op jit(solution)/shard_map/ppermute | solution.py:17
  19.3 2.4 %copy.18 = bf16[1,256,48,128]{3,1,2,0:T(8,128)(2,1)} copy(bf16[1,256,48,128]{3,2,1,0:T(8,128)(2,1)S(1)} %copy-done) | data formatting | bytes 6291456 | tf_op args[0]
  21.7 2.8 %copy.17 = bf16[1,256,48,1]{3,1,2,0:T(8,128)(2,1)} copy(bf16[1,256,48,1]{1,2,3,0:T(8,128)(2,1)S(1)} %collective-permute-done) | data formatting | bytes 49152 | tf_op jit(solution)/shard_map/ppermute | solution.py:16
  24.5 2.8 %copy.19 = bf16[1,256,48,1]{3,1,2,0:T(8,128)(2,1)} copy(bf16[1,256,48,1]{1,2,3,0:T(8,128)(2,1)S(1)} %collective-permute-done.1) | data formatting | bytes 49152 | tf_op jit(solution)/shard_map/ppermute | solution.py:17
  27.3 1.3 pad_maximum_fusion.2
  28.6 4.4 %collective-permute-start.2 = (bf16[1,256,1,130]{3,1,2,0:T(8,128)(2,1)S(1)}, bf16[1,256,1,130]{3,1,2,0:T(8,128)(2,1)S(1)}, u32[]{:S(2)}, u32[]{:S(2)}) collective-permute-start(bf16[1,256,1,130]{3,1,2,0:T(8,128)(2,1)S(1)} %get-tuple-element.111), channel_id=1, source_target_pairs={{0,4},{4,8},{8,12},{1,5},{5,9},{9,13},{2,6},{6,10},{10,14},{3,7},{... | collective-permute-start | bytes 199688 | tf_op jit(solution)/shard_map/ppermute | solution.py:16
  33.0 0.0 copy-start.6
  33.0 1.6 collective-permute-start.3
  34.6 1.2 collective-permute-done.2
  35.7 4.3 %collective-permute-done.3 = bf16[1,256,1,130]{3,1,2,0:T(8,128)(2,1)S(1)} collective-permute-done((bf16[1,256,1,130]{3,1,2,0:T(8,128)(2,1)S(1)}, bf16[1,256,1,130]{3,1,2,0:T(8,128)(2,1)S(1)}, u32[]{:S(2)}, u32[]{:S(2)}) %collective-permute-start.3) | collective-permute-done | bytes 66592 | tf_op jit(solution)/shard_map/ppermute | solution.py:17
  40.0 6.6 %maximum_bitcast_fusion = bf16[256,50,130]{2,0,1:T(8,128)(2,1)S(1)} fusion(bf16[1,256,1,130]{3,1,2,0:T(8,128)(2,1)S(1)} %collective-permute-done.3, bf16[1,256,48,1]{3,1,2,0:T(8,128)(2,1)S(1)} %copy-done.3, bf16[1,256,48,128]{3,1,2,0:T(8,128)(2,1)S(1)} %copy-done.1, bf16[1,256,48,1]{3,1,2,0:T(8,128)(2,1)S(1)} %copy-done.2, ...), kind=kLoop, calls=%fused_computation.2 | loop fusion | flops 16640000 | bytes 6656000 | tf_op jit(solution)/shard_map/squeeze | solution.py:61
  46.6 1.2 fusion.3
  47.9 0.7 fusion.5
  48.5 1.2 fusion.7
  49.8 1.2 fusion.9
  51.0 0.7 fusion.11
  51.7 1.2 fusion.13
  52.9 1.2 fusion.15
  54.1 0.7 fusion.17
  54.8 2.7 %add_convert_fusion.1 = bf16[48,128,69]{1,2,0:T(8,128)(2,1)} fusion(f32[48,128,69]{1,2,0:T(8,128)S(1)} %fusion.3, f32[48,128,69]{1,2,0:T(8,128)S(1)} %fusion.5, f32[48,128,69]{1,2,0:T(8,128)S(1)} %fusion.7, f32[48,128,69]{1,2,0:T(8,128)S(1)} %fusion.9, f32[48,128,69]{1,2,0:T(8,128)S(1)} %fusion.11, f32[48,128,69]{1,2,0:T(8,128)S(1)} %fusion.13, ...), kind=kOutput, calls=%fused_computation.27 | convolution fusion | flops 221294592 | bytes 18186752 | tf_op jit(solution)/shard_map/dot_general | solution.py:66
  57.5 3.8 %all-to-all-start = ((bf16[1,69,48,128]{3,1,0,2:T(8,128)(2,1)}), bf16[1,69,48,128]{3,1,0,2:T(8,128)(2,1)S(1)}, u32[]{:S(2)}, u32[]{:S(2)}) async-start(bf16[1,69,48,128]{3,1,0,2:T(8,128)(2,1)} %bitcast.22), calls=%async_computation | async-start | bytes 1769472 | tf_op jit(solution)/shard_map/all_to_all | solution.py:76
  61.3 10.8 %all-to-all-done = bf16[1,69,48,128]{3,1,0,2:T(8,128)(2,1)S(1)} async-done(((bf16[1,69,48,128]{3,1,0,2:T(8,128)(2,1)}), bf16[1,69,48,128]{3,1,0,2:T(8,128)(2,1)S(1)}, u32[]{:S(2)}, u32[]{:S(2)}) %all-to-all-start) | async-done | bytes 847904 | tf_op jit(solution)/shard_map/all_to_all | solution.py:76
  72.1 0.2 fusion.78
  72.3 4.8 %while.14 = (s32[]{:T(128)}, f32[2,69,24,128]{3,2,1,0:T(8,128)}, bf16[2,69,24,128]{3,2,1,0:T(8,128)(2,1)S(1)}, f32[2,69,24,128]{3,2,1,0:T(8,128)S(1)}, s32[]{:T(128)}, /*index=5*/s32[]{:T(128)}) while((s32[]{:T(128)}, f32[2,69,24,128]{3,2,1,0:T(8,128)}, bf16[2,69,24,128]{3,2,1,0:T(8,128)(2,1)S(1)}, ...), condition=%wide.region_1.2_spmd.clone, body=%wide.region_0.1_spmd.clone.sunk | while | flops 2755587 | bytes 7207003 | solution.py:39
  72.3 0.1 bitcast_convert_fusion.2
  72.4 1.6 select_add_fusion.2
  74.0 0.1 bitcast_convert_fusion.2
  74.0 3.0 %select_add_fusion.2 = f32[2,69,24,128]{3,2,1,0:T(8,128)} fusion(f32[2,69,24,128]{3,2,1,0:T(8,128)} %get-tuple-element.151, f32[2,69,24,128]{3,2,1,0:T(8,128)S(1)} %get-tuple-element.159, f32[69,24,128]{2,1,0:T(8,128)S(1)} %bitcast_convert_fusion.2, pred[]{:T(512)S(6)} %compare.3), kind=kLoop, calls=%fused_computation.clone.1 | loop fusion | flops 2543616 | bytes 5935105 | tf_op jit(solution)/shard_map/while/body/eval_jaxpr/add | solution.py:37
  77.1 3.8 %all-to-all-start.1 = ((f32[2,69,24,128]{3,2,1,0:T(8,128)}), f32[2,69,24,128]{3,2,1,0:T(8,128)S(1)}, u32[]{:S(2)}, u32[]{:S(2)}) async-start(f32[2,69,24,128]{3,2,1,0:T(8,128)} %get-tuple-element.81), calls=%async_computation.1 | async-start | bytes 3391488 | tf_op jit(solution)/shard_map/all_to_all | solution.py:78
  81.0 0.1 broadcast_multiply_fusion
  81.0 18.7 %all-to-all-done.1 = f32[2,69,24,128]{3,2,1,0:T(8,128)S(1)} async-done(((f32[2,69,24,128]{3,2,1,0:T(8,128)}), f32[2,69,24,128]{3,2,1,0:T(8,128)S(1)}, u32[]{:S(2)}, u32[]{:S(2)}) %all-to-all-start.1) | async-done | bytes 1695776 | tf_op jit(solution)/shard_map/all_to_all | solution.py:78
  99.8 0.3 copy.23
  100.1 2.1 %fusion.20 = bf16[69,48,128]{2,0,1:T(8,128)(2,1)S(1)} fusion(f32[1,69,2,24,128]{4,1,3,2,0:T(8,128)S(1)} %copy.23, bf16[48,128,69]{1,2,0:T(8,128)(2,1)} %add_convert_fusion.1, bf16[69,48,128]{2,1,0:T(8,128)(2,1)} %param.10, f32[69,48]{0,1:T(8,128)S(1)} %broadcast_multiply_fusion), kind=kLoop, calls=%fused_computation.26 | loop fusion | flops 3815424 | bytes 4252608 | tf_op jit(solution)/shard_map/convert_element_type | solution.py:85
  102.2 0.3 fusion.80
  102.6 0.4 copy.24
  103.0 0.0 collective-permute-start.4
  103.0 0.4 copy.25
  103.5 1.8 collective-permute-start.5
  105.2 0.9 collective-permute-done.4
  106.1 0.5 copy.26
  106.7 0.5 copy.27
  107.2 0.0 copy-start.5
  107.2 0.1 pad_maximum_fusion.5
  107.3 3.5 %collective-permute-start.6 = (bf16[1,69,1,130]{3,1,2,0:T(8,128)(2,1)S(1)}, bf16[1,69,1,130]{3,1,2,0:T(8,128)(2,1)S(1)}, u32[]{:S(2)}, u32[]{:S(2)}) collective-permute-start(bf16[1,69,1,130]{3,1,2,0:T(8,128)(2,1)S(1)} %get-tuple-element.115), channel_id=1, source_target_pairs={{0,4},{4,8},{8,12},{1,5},{5,9},{9,13},{2,6},{6,10},{10,14},{3,7},{... | collective-permute-start | bytes 53828 | tf_op jit(solution)/shard_map/ppermute | solution.py:16
  110.8 1.3 collective-permute-start.7
  112.1 0.0 copy-start.7
  112.1 2.2 %copy.28 = bf16[1,69,48,128]{3,2,1,0:T(8,128)(2,1)} copy(bf16[1,69,48,128]{3,1,2,0:T(8,128)(2,1)} %bitcast.20) | data formatting | bytes 1695744
  114.3 0.0 collective-permute-done.6
  114.3 2.3 %collective-permute-done.7 = bf16[1,69,1,130]{3,1,2,0:T(8,128)(2,1)S(1)} collective-permute-done((bf16[1,69,1,130]{3,1,2,0:T(8,128)(2,1)S(1)}, bf16[1,69,1,130]{3,1,2,0:T(8,128)(2,1)S(1)}, u32[]{:S(2)}, u32[]{:S(2)}) %collective-permute-start.7) | collective-permute-done | bytes 17972 | tf_op jit(solution)/shard_map/ppermute | solution.py:17
  116.6 2.4 %maximum_bitcast_fusion.1 = bf16[69,50,130]{2,0,1:T(8,128)(2,1)S(1)} fusion(bf16[1,69,1,130]{3,1,2,0:T(8,128)(2,1)S(1)} %collective-permute-done.7, bf16[1,69,48,1]{3,1,2,0:T(8,128)(2,1)} %copy-done.5, bf16[1,69,48,128]{3,1,2,0:T(8,128)(2,1)S(1)} %bitcast.102, bf16[1,69,48,1]{3,1,2,0:T(8,128)(2,1)} %copy-done.4, ...), kind=kLoop, calls=%fused_computation.23 | loop fusion | flops 4485000 | bytes 1794000 | tf_op jit(solution)/shard_map/squeeze | solution.py:86
  119.1 4.5 %fusion.22 = f32[48,128,256]{2,1,0:T(8,128)} fusion(bf16[69,50,130]{2,0,1:T(8,128)(2,1)S(1)} %maximum_bitcast_fusion.1, bf16[3,3,69,256]{3,2,1,0:T(8,128)(2,1)S(1)} %copy-done.7), kind=kOutput, calls=%fused_computation.29 | convolution fusion | flops 217055232 | bytes 7213056 | tf_op jit(solution)/shard_map/dot_general | solution.py:93
  123.6 4.5 %fusion.24 = f32[48,128,256]{2,1,0:T(8,128)} fusion(bf16[69,50,130]{2,0,1:T(8,128)(2,1)S(1)} %maximum_bitcast_fusion.1, bf16[3,3,69,256]{3,2,1,0:T(8,128)(2,1)S(1)} %copy-done.7), kind=kOutput, calls=%fused_computation.31 | convolution fusion | flops 217055232 | bytes 7213056 | tf_op jit(solution)/shard_map/dot_general | solution.py:93
  128.1 3.6 %fusion.26 = f32[48,128,256]{2,1,0:T(8,128)} fusion(bf16[69,50,130]{2,0,1:T(8,128)(2,1)S(1)} %maximum_bitcast_fusion.1, bf16[3,3,69,256]{3,2,1,0:T(8,128)(2,1)S(1)} %copy-done.7), kind=kOutput, calls=%fused_computation.33 | convolution fusion | flops 217055232 | bytes 7213056 | tf_op jit(solution)/shard_map/dot_general | solution.py:93
  131.7 4.5 %fusion.28 = f32[48,128,256]{2,1,0:T(8,128)} fusion(bf16[69,50,130]{2,0,1:T(8,128)(2,1)S(1)} %maximum_bitcast_fusion.1, bf16[3,3,69,256]{3,2,1,0:T(8,128)(2,1)S(1)} %copy-done.7), kind=kOutput, calls=%fused_computation.35 | convolution fusion | flops 217055232 | bytes 7213056 | tf_op jit(solution)/shard_map/dot_general | solution.py:93
  136.2 4.6 %fusion.30 = f32[48,128,256]{2,1,0:T(8,128)} fusion(bf16[69,50,130]{2,0,1:T(8,128)(2,1)S(1)} %maximum_bitcast_fusion.1, bf16[3,3,69,256]{3,2,1,0:T(8,128)(2,1)S(1)} %copy-done.7), kind=kOutput, calls=%fused_computation.37 | convolution fusion | flops 217055232 | bytes 7213056 | tf_op jit(solution)/shard_map/dot_general | solution.py:93
  140.8 3.8 %fusion.32 = f32[48,128,256]{2,1,0:T(8,128)} fusion(bf16[69,50,130]{2,0,1:T(8,128)(2,1)S(1)} %maximum_bitcast_fusion.1, bf16[3,3,69,256]{3,2,1,0:T(8,128)(2,1)S(1)} %copy-done.7), kind=kOutput, calls=%fused_computation.39 | convolution fusion | flops 217055232 | bytes 7213056 | tf_op jit(solution)/shard_map/dot_general | solution.py:93
  144.6 4.5 %fusion.34 = f32[48,128,256]{2,1,0:T(8,128)} fusion(bf16[69,50,130]{2,0,1:T(8,128)(2,1)S(1)} %maximum_bitcast_fusion.1, bf16[3,3,69,256]{3,2,1,0:T(8,128)(2,1)S(1)} %copy-done.7), kind=kOutput, calls=%fused_computation.41 | convolution fusion | flops 217055232 | bytes 7213056 | tf_op jit(solution)/shard_map/dot_general | solution.py:93
  149.0 4.5 %fusion.36 = f32[48,128,256]{2,1,0:T(8,128)} fusion(bf16[69,50,130]{2,0,1:T(8,128)(2,1)S(1)} %maximum_bitcast_fusion.1, bf16[3,3,69,256]{3,2,1,0:T(8,128)(2,1)S(1)} %copy-done.7), kind=kOutput, calls=%fused_computation.43 | convolution fusion | flops 217055232 | bytes 7213056 | tf_op jit(solution)/shard_map/dot_general | solution.py:93
  153.5 18.4 %fusion = bf16[1,256,48,128]{1,3,2,0:T(8,128)(2,1)} fusion(f32[48,128,256]{2,1,0:T(8,128)} %fusion.22, f32[48,128,256]{2,1,0:T(8,128)} %fusion.24, f32[48,128,256]{2,1,0:T(8,128)} %fusion.26, f32[48,128,256]{2,1,0:T(8,128)} %fusion.28, f32[48,128,256]{2,1,0:T(8,128)} %fusion.30, f32[48,128,256]{2,1,0:T(8,128)} %fusion.32, f32[48,128,256]{2,1,0:T(8,128)} %fusion.36, ...), kind=kOutput, calls=%fused_computation.4 | convolution fusion | flops 231211008 | bytes 54398976 | tf_op jit(solution)/shard_map/dot_general | solution.py:93
  171.9 4.8 %copy.29 = bf16[1,256,48,128]{3,2,1,0:T(8,128)(2,1)} copy(bf16[1,256,48,128]{1,3,2,0:T(8,128)(2,1)} %fusion) | data formatting | bytes 6291456
  (22 shorter events, 0.1 us)
Async XLA Ops:
  7.5 11.8 %copy-start = (bf16[1,256,48,128]{3,2,1,0:T(8,128)(2,1)S(1)}, bf16[1,256,48,128]{3,2,1,0:T(8,128)(2,1)}, u32[]{:S(2)}) copy-start(bf16[1,256,48,128]{3,2,1,0:T(8,128)(2,1)} %param.7) | copy-start | bytes 9437188
  12.2 9.5 %collective-permute-start = (bf16[1,256,48,1]{1,2,3,0:T(8,128)(2,1)S(1)}, bf16[1,256,48,1]{1,2,3,0:T(8,128)(2,1)S(1)}, u32[]{:S(2)}, u32[]{:S(2)}) collective-permute-start(bf16[1,256,48,1]{1,2,3,0:T(8,128)(2,1)S(1)} %copy.30), channel_id=1, source_target_pairs={{0,1},{1,2},{2,3},{3,0},{4,5},{5,6},{6,7},{7,4},{8,9},{9,10},{10,1... | collective-permute-start | bytes 73736 | tf_op jit(solution)/shard_map/ppermute | solution.py:16
  17.3 7.2 %collective-permute-start.1 = (bf16[1,256,48,1]{1,2,3,0:T(8,128)(2,1)S(1)}, bf16[1,256,48,1]{1,2,3,0:T(8,128)(2,1)S(1)}, u32[]{:S(2)}, u32[]{:S(2)}) collective-permute-start(bf16[1,256,48,1]{1,2,3,0:T(8,128)(2,1)S(1)} %copy.31), channel_id=1, source_target_pairs={{1,0},{2,1},{3,2},{0,3},{5,4},{6,5},{7,6},{4,7},{9,8},{10,9},{11,1... | collective-permute-start | bytes 73736 | tf_op jit(solution)/shard_map/ppermute | solution.py:17
  21.7 5.6 %copy-start.1 = (bf16[1,256,48,128]{3,1,2,0:T(8,128)(2,1)S(1)}, bf16[1,256,48,128]{3,1,2,0:T(8,128)(2,1)}, u32[]{:S(2)}) copy-start(bf16[1,256,48,128]{3,1,2,0:T(8,128)(2,1)} %copy.18) | copy-start | bytes 9437188
  27.3 12.7 %copy-start.2 = (bf16[1,256,48,1]{3,1,2,0:T(8,128)(2,1)S(1)}, bf16[1,256,48,1]{3,1,2,0:T(8,128)(2,1)}, u32[]{:S(2)}) copy-start(bf16[1,256,48,1]{3,1,2,0:T(8,128)(2,1)} %copy.17) | copy-start | bytes 73732
  27.3 12.7 %copy-start.3 = (bf16[1,256,48,1]{3,1,2,0:T(8,128)(2,1)S(1)}, bf16[1,256,48,1]{3,1,2,0:T(8,128)(2,1)}, u32[]{:S(2)}) copy-start(bf16[1,256,48,1]{3,1,2,0:T(8,128)(2,1)} %copy.19) | copy-start | bytes 73732
  28.6 7.2 %collective-permute-start.2 = (bf16[1,256,1,130]{3,1,2,0:T(8,128)(2,1)S(1)}, bf16[1,256,1,130]{3,1,2,0:T(8,128)(2,1)S(1)}, u32[]{:S(2)}, u32[]{:S(2)}) collective-permute-start(bf16[1,256,1,130]{3,1,2,0:T(8,128)(2,1)S(1)} %get-tuple-element.111), channel_id=1, source_target_pairs={{0,4},{4,8},{8,12},{1,5},{5,9},{9,13},{2,6},{6,10},{10,14},{3,7},{... | collective-permute-start | bytes 199688 | tf_op jit(solution)/shard_map/ppermute | solution.py:16
  33.0 13.7 %copy-start.6 = (bf16[3,3,69,256]{3,2,1,0:T(8,128)(2,1)S(1)}, bf16[3,3,69,256]{3,2,1,0:T(8,128)(2,1)}, u32[]{:S(2)}) copy-start(bf16[3,3,69,256]{3,2,1,0:T(8,128)(2,1)} %param.8) | copy-start | bytes 953860
  33.0 7.0 %collective-permute-start.3 = (bf16[1,256,1,130]{3,1,2,0:T(8,128)(2,1)S(1)}, bf16[1,256,1,130]{3,1,2,0:T(8,128)(2,1)S(1)}, u32[]{:S(2)}, u32[]{:S(2)}) collective-permute-start(bf16[1,256,1,130]{3,1,2,0:T(8,128)(2,1)S(1)} %get-tuple-element.112), channel_id=1, source_target_pairs={{4,0},{8,4},{12,8},{5,1},{9,5},{13,9},{6,2},{10,6},{14,10},{7,3},{... | collective-permute-start | bytes 199688 | tf_op jit(solution)/shard_map/ppermute | solution.py:17
  54.1 0.7 copy-start.8
  57.5 14.6 %all-to-all-start = ((bf16[1,69,48,128]{3,1,0,2:T(8,128)(2,1)}), bf16[1,69,48,128]{3,1,0,2:T(8,128)(2,1)S(1)}, u32[]{:S(2)}, u32[]{:S(2)}) async-start(bf16[1,69,48,128]{3,1,0,2:T(8,128)(2,1)} %bitcast.22), calls=%async_computation | async-start | bytes 1769472 | tf_op jit(solution)/shard_map/all_to_all | solution.py:76
  77.1 3.9 %copy-start.9 = (f32[69]{0:T(128)S(1)}, f32[69]{0:T(128)}, u32[]{:S(2)}) copy-start(f32[69]{0:T(128)} %param.11) | copy-start | bytes 832
  77.1 22.7 %all-to-all-start.1 = ((f32[2,69,24,128]{3,2,1,0:T(8,128)}), f32[2,69,24,128]{3,2,1,0:T(8,128)S(1)}, u32[]{:S(2)}, u32[]{:S(2)}) async-start(f32[2,69,24,128]{3,2,1,0:T(8,128)} %get-tuple-element.81), calls=%async_computation.1 | async-start | bytes 3391488 | tf_op jit(solution)/shard_map/all_to_all | solution.py:78
  103.0 3.2 %collective-permute-start.4 = (bf16[1,69,48,1]{1,2,3,0:T(8,128)(2,1)S(1)}, bf16[1,69,48,1]{1,2,3,0:T(8,128)(2,1)S(1)}, u32[]{:S(2)}, u32[]{:S(2)}) collective-permute-start(bf16[1,69,48,1]{1,2,3,0:T(8,128)(2,1)S(1)} %copy.24), channel_id=1, source_target_pairs={{0,1},{1,2},{2,3},{3,0},{4,5},{5,6},{6,7},{7,4},{8,9},{9,10},{10,1... | collective-permute-start | bytes 19880 | tf_op jit(solution)/shard_map/ppermute | solution.py:16
  103.5 3.2 %collective-permute-start.5 = (bf16[1,69,48,1]{1,2,3,0:T(8,128)(2,1)S(1)}, bf16[1,69,48,1]{1,2,3,0:T(8,128)(2,1)S(1)}, u32[]{:S(2)}, u32[]{:S(2)}) collective-permute-start(bf16[1,69,48,1]{1,2,3,0:T(8,128)(2,1)S(1)} %copy.25), channel_id=1, source_target_pairs={{1,0},{2,1},{3,2},{0,3},{5,4},{6,5},{7,6},{4,7},{9,8},{10,9},{11,1... | collective-permute-start | bytes 19880 | tf_op jit(solution)/shard_map/ppermute | solution.py:17
  106.6 7.7 %copy-start.4 = (bf16[1,69,48,1]{3,1,2,0:T(8,128)(2,1)}, bf16[1,69,48,1]{3,1,2,0:T(8,128)(2,1)S(1)}, u32[]{:S(2)}) copy-start(bf16[1,69,48,1]{3,1,2,0:T(8,128)(2,1)S(1)} %copy.26) | copy-start | bytes 19876
  107.2 7.2 %copy-start.5 = (bf16[1,69,48,1]{3,1,2,0:T(8,128)(2,1)}, bf16[1,69,48,1]{3,1,2,0:T(8,128)(2,1)S(1)}, u32[]{:S(2)}) copy-start(bf16[1,69,48,1]{3,1,2,0:T(8,128)(2,1)S(1)} %copy.27) | copy-start | bytes 19876
  107.3 7.0 %collective-permute-start.6 = (bf16[1,69,1,130]{3,1,2,0:T(8,128)(2,1)S(1)}, bf16[1,69,1,130]{3,1,2,0:T(8,128)(2,1)S(1)}, u32[]{:S(2)}, u32[]{:S(2)}) collective-permute-start(bf16[1,69,1,130]{3,1,2,0:T(8,128)(2,1)S(1)} %get-tuple-element.115), channel_id=1, source_target_pairs={{0,4},{4,8},{8,12},{1,5},{5,9},{9,13},{2,6},{6,10},{10,14},{3,7},{... | collective-permute-start | bytes 53828 | tf_op jit(solution)/shard_map/ppermute | solution.py:16
  110.8 5.9 %collective-permute-start.7 = (bf16[1,69,1,130]{3,1,2,0:T(8,128)(2,1)S(1)}, bf16[1,69,1,130]{3,1,2,0:T(8,128)(2,1)S(1)}, u32[]{:S(2)}, u32[]{:S(2)}) collective-permute-start(bf16[1,69,1,130]{3,1,2,0:T(8,128)(2,1)S(1)} %get-tuple-element.116), channel_id=1, source_target_pairs={{4,0},{8,4},{12,8},{5,1},{9,5},{13,9},{6,2},{10,6},{14,10},{7,3},{... | collective-permute-start | bytes 53828 | tf_op jit(solution)/shard_map/ppermute | solution.py:17
  112.1 7.0 %copy-start.7 = (bf16[3,3,69,256]{3,2,1,0:T(8,128)(2,1)S(1)}, bf16[3,3,69,256]{3,2,1,0:T(8,128)(2,1)}, u32[]{:S(2)}) copy-start(bf16[3,3,69,256]{3,2,1,0:T(8,128)(2,1)} %param.8) | copy-start | bytes 953860
where the time goes:
time: 177 us
  matrix products  63.7 us (36%)
  waiting for transfers between devices  38.1 us (22%)
  local copies, waits for them, and re-layouts  33.7 us (19%)
  starting transfers between devices  22.7 us (13%)
  other arithmetic  17.6 us (10%)
    dot_general x9, matrix products, shards(): lax.dot_general(conv_weight[row_tap, col_tap], window, (((0,), (0,)), (()...  52.9 us
    unnamed x25, local copies, waits for them, and re-layouts  18.8 us
    all_to_all x1, waiting for transfers between devices, shards(): lax.all_to_all(pair_block, 'member', split_axis=0, concat_axis=2, tiled=T...  18.7 us
    dot_general x9, matrix products, shards(): lax.dot_general(conv_weight[row_tap, col_tap], window, (((1,), (0,)), (()...  10.8 us
    all_to_all x1, waiting for transfers between devices, shards(): lax.all_to_all(predicted_fields, 'member', split_axis=2, concat_axis=0, t...  10.8 us
    ppermute x4, starting transfers between devices, extended(): before = lax.ppermute(last, axis, up)  8.47 us
    slice x3, local copies, waits for them, and re-layouts, extended(): last = lax.slice_in_dim(shard, length - width, length, axis=dim)  7.67 us
    ppermute x4, starting transfers between devices, extended(): after = lax.ppermute(initial, axis, down)  6.65 us
  transfers between devices with their start and end apart: 10, of which 6 were waited for; matrix products, arithmetic and copies ran while one was open for 7% of the time, Pallas kernels for 0%

commit v1 on v0

v1 whole, which is shorter than its diff:
```python
import functools

import jax
import jax.numpy as jnp
from jax import lax
from jax.experimental import pallas as pl
from jax.experimental.pallas import tpu as pltpu
from jax.sharding import PartitionSpec as P

MESH = pl.DeviceIdType.MESH
smoothing = 0.25
CHUNK = 16
f32, bf16 = jnp.float32, jnp.bfloat16


def smooth(difference):
    return difference * lax.rsqrt(difference * difference + smoothing * smoothing)


def kernel(
    sizes,
    x_ref, w_ref, obs_ref, bias_ref, var_ref,
    p_ref, out_ref,
    big, xt, wf, wbt, wb, pf, g, gs, others, latw,
    edge_out, edge_in, gedge_out, gedge_in,
    row_send, row_recv, grow_send, grow_recv,
    edge_send, edge_recv, gedge_send, gedge_recv, peer_send, peer_recv,
):
    members, lats, lons, channels, rows, cols, outputs, padded = sizes
    chunks = rows // CHUNK
    order = [0] + ([chunks - 1] if chunks > 1 else []) + list(range(1, chunks - 1))
    me, lat, lon = lax.axis_index("member"), lax.axis_index("lat"), lax.axis_index("lon")
    right, left = lax.rem(lon + 1, lons), lax.rem(lon + lons - 1, lons)
    has_up, has_down = lat > 0, lat < lats - 1

    barrier = pltpu.get_barrier_semaphore()
    for side in (left, right):
        pl.semaphore_signal(barrier, inc=1, device_id=(me, lat, side), device_id_type=MESH)

    @pl.when(has_up)
    def _():
        pl.semaphore_signal(barrier, inc=1, device_id=(me, lat - 1, lon), device_id_type=MESH)

    @pl.when(has_down)
    def _():
        pl.semaphore_signal(barrier, inc=1, device_id=(me, lat + 1, lon), device_id_type=MESH)

    def greet(step, carry):
        other = lax.rem(me + step, members)
        pl.semaphore_signal(barrier, inc=1, device_id=(other, lat, lon), device_id_type=MESH)
        return carry

    lax.fori_loop(1, members, greet, 0)

    def widen(c, carry):
        start = pl.multiple_of(c * rows, rows)
        big[pl.ds(start, rows), :] = x_ref[c].astype(f32)
        return carry

    lax.fori_loop(0, channels, widen, 0, unroll=4)

    def turn(r, carry):
        xt[r + 1] = big[pl.ds(r, channels, stride=rows), :].astype(bf16)
        return carry

    turn(0, 0)
    turn(rows - 1, 0)
    pl.semaphore_wait(barrier, members + 1 + has_up.astype(jnp.int32) + has_down.astype(jnp.int32))

    def row_copies(array, send, recv):
        up = pltpu.make_async_remote_copy(
            src_ref=array.at[1], dst_ref=array.at[rows + 1], send_sem=send.at[0],
            recv_sem=recv.at[0], device_id=(me, lat - 1, lon), device_id_type=MESH)
        down = pltpu.make_async_remote_copy(
            src_ref=array.at[rows], dst_ref=array.at[0], send_sem=send.at[1],
            recv_sem=recv.at[1], device_id=(me, lat + 1, lon), device_id_type=MESH)
        return up, down

    def start_up(copies):
        pl.when(has_up)(lambda: copies[0].start())

    def start_down(copies):
        pl.when(has_down)(lambda: copies[1].start())

    def wait_rows(copies, array):
        @pl.when(has_up)
        def _():
            copies[1].wait_recv()
            copies[0].wait_send()

        @pl.when(has_down)
        def _():
            copies[0].wait_recv()
            copies[1].wait_send()

        @pl.when(lat == 0)
        def _():
            array[0] = jnp.zeros(array.shape[1:], bf16)

        @pl.when(lat == lats - 1)
        def _():
            array[rows + 1] = jnp.zeros(array.shape[1:], bf16)

    x_rows = row_copies(xt, row_send, row_recv)
    start_up(x_rows)
    start_down(x_rows)
    lax.fori_loop(1, rows - 1, turn, 0)

    wf[...] = jnp.zeros(wf.shape, bf16)
    for a in range(3):
        for b in range(3):
            wf[b * padded : b * padded + outputs, a * channels : (a + 1) * channels] = w_ref[a, b]

    lane = lax.broadcasted_iota(jnp.int32, (padded, cols), 1)

    def forward(pair, q):
        rhs = jnp.concatenate(
            [xt[pl.ds(2 * pair + i, 3)].reshape(3 * channels, cols) for i in range(2)], axis=1)
        y = jnp.dot(wf[...], rhs, preferred_element_type=f32)
        for i in range(2):
            r = 2 * pair + i
            from_left, mid, from_right = [
                y[b * padded : (b + 1) * padded, i * cols : (i + 1) * cols] for b in range(3)]
            from_left = pltpu.roll(from_left, 1, 1)
            from_right = pltpu.roll(from_right, cols - 1, 1)
            edge_out[q, 0] = jnp.where(lane == r, pltpu.roll(from_left, r, 1), edge_out[q, 0])
            edge_out[q, 1] = jnp.where(lane == r, pltpu.roll(from_right, r + 1, 1), edge_out[q, 1])
            total = mid + jnp.where(lane == 0, 0.0, from_left)
            total = total + jnp.where(lane == cols - 1, 0.0, from_right)
            pf[pl.ds(r, padded, stride=rows), :] = total

    def edge_copies(q, source, target, send, recv):
        return [
            pltpu.make_async_remote_copy(
                src_ref=source.at[q, s], dst_ref=target.at[q, s], send_sem=send.at[q, s],
                recv_sem=recv.at[q, s], device_id=(me, lat, side), device_id_type=MESH)
            for s, side in enumerate((right, left))]

    def run_pairs(pairs, body):
        pairs = sorted(pairs)
        while pairs:
            n = 1
            while n < len(pairs) and pairs[n] == pairs[0] + n:
                n += 1

            def step(pair, carry):
                body(pair)
                return carry

            lax.fori_loop(pairs[0], pairs[0] + n, step, 0)
            pairs = pairs[n:]

    peer = lambda q, step: pltpu.make_async_remote_copy(
        src_ref=p_ref.at[:, pl.ds(q * CHUNK, CHUNK), :],
        dst_ref=others.at[step - 1, :, pl.ds(q * CHUNK, CHUNK), :],
        send_sem=peer_send.at[q, step - 1], recv_sem=peer_recv.at[q, step - 1],
        device_id=(lax.rem(me + step, members), lat, lon), device_id_type=MESH)

    edges = {}

    def finish(q):
        for copy in edges[q]:
            copy.wait()

        def fix(r, carry):
            at = pl.ds(r, padded, stride=rows)
            left_edge = pltpu.roll(edge_in[q, 0], lax.rem(cols - r, cols), 1)
            right_edge = pltpu.roll(edge_in[q, 1], cols - 1 - r, 1)
            total = pf[at, :]
            total = total + jnp.where(lane == 0, left_edge, 0.0)
            pf[at, :] = total + jnp.where(lane == cols - 1, right_edge, 0.0)
            return carry

        lax.fori_loop(q * CHUNK, (q + 1) * CHUNK, fix, 0)

        def pack(o, carry):
            at = pl.ds(pl.multiple_of(o * rows + q * CHUNK, CHUNK), CHUNK)
            p_ref[o, q * CHUNK : (q + 1) * CHUNK, :] = (pf[at, :] + bias_ref[o]).astype(bf16)
            return carry

        lax.fori_loop(0, outputs, pack, 0, unroll=3)

        def send(step, carry):
            peer(q, step).start()
            return carry

        lax.fori_loop(1, members, send, 0)

    half = CHUNK // 2
    waited = False
    for at, q in enumerate(order):
        edge_out[q] = jnp.zeros(edge_out.shape[1:], f32)
        pairs = range(q * half, (q + 1) * half)
        bounds = [p for p in pairs if p in (0, rows // 2 - 1)]
        run_pairs([p for p in pairs if p not in bounds], lambda p: forward(p, q))
        if bounds and not waited:
            wait_rows(x_rows, xt)
            waited = True
        for p in bounds:
            forward(p, q)
        edges[q] = edge_copies(q, edge_out, edge_in, edge_send, edge_recv)
        for copy in edges[q]:
            copy.start()
        if at:
            finish(order[at - 1])
    finish(order[-1])

    wbt[...] = jnp.zeros(wbt.shape, bf16)
    for a in range(3):
        for b in range(3):
            base = ((2 - a) * 3 + b) * padded
            wbt[base : base + outputs, :] = w_ref[a, b]
    wb[...] = jnp.transpose(wbt[...])
    row_index = (lat * rows + lax.broadcasted_iota(jnp.int32, (rows, cols), 0)).astype(f32)
    latw[...] = jnp.cos((-80.0 + 160.0 * (row_index + 0.5) / float(rows * lats)) * (jnp.pi / 180.0))

    def misfit(o, carry):
        at = pl.ds(pl.multiple_of(o * rows, rows), rows)
        g[at, :] = smooth(p_ref[o].astype(f32) - obs_ref[o].astype(f32))
        return carry

    lax.fori_loop(0, outputs, misfit, 0, unroll=3)
    g[pl.ds(outputs * rows, (padded - outputs) * rows), :] = jnp.zeros(
        ((padded - outputs) * rows, cols), f32)

    def gradient(q):
        inside = slice(q * CHUNK, (q + 1) * CHUNK)

        def arrive(step, carry):
            peer(q, step).wait()
            return carry

        lax.fori_loop(1, members, arrive, 0)
        weight_row = latw[inside, :]

        def score(o, carry):
            at = pl.ds(pl.multiple_of(o * rows + q * CHUNK, CHUNK), CHUNK)
            own = p_ref[o, inside, :].astype(f32)
            add = lambda j, run: run + smooth(own - others[j, o, inside, :].astype(f32))
            pair_sum = smooth(own - own)
            if members == 2:
                pair_sum = add(0, pair_sum)
            else:
                pair_sum = lax.fori_loop(0, members - 1, add, pair_sum)
            value = weight_row * var_ref[o] * (g[at, :] - pair_sum / (members - 1))
            g[at, :] = value.astype(bf16).astype(f32)
            return carry

        lax.fori_loop(0, outputs, score, 0, unroll=3)

        def collect(r, carry):
            to_right, to_left = carry
            row = g[pl.ds(r, padded, stride=rows), :]
            to_right = jnp.where(lane == r, pltpu.roll(row, r + 1, 1), to_right)
            to_left = jnp.where(lane == r, pltpu.roll(row, r, 1), to_left)
            return to_right, to_left

        zero = jnp.zeros((padded, cols), f32)
        gedge_out[q, 0], gedge_out[q, 1] = lax.fori_loop(
            q * CHUNK, (q + 1) * CHUNK, collect, (zero, zero))
        copies = edge_copies(q, gedge_out, gedge_in, gedge_send, gedge_recv)
        for copy in copies:
            copy.start()
        return copies

    def shifted(q):
        def one(r, carry):
            row = g[pl.ds(r, padded, stride=rows), :]
            left_edge = pltpu.roll(gedge_in[q, 0], lax.rem(cols - r, cols), 1)
            right_edge = pltpu.roll(gedge_in[q, 1], cols - 1 - r, 1)
            ahead = jnp.where(lane == cols - 1, right_edge, pltpu.roll(row, cols - 1, 1))
            behind = jnp.where(lane == 0, left_edge, pltpu.roll(row, 1, 1))
            gs[r + 1, 0:padded, :] = ahead.astype(bf16)
            gs[r + 1, padded : 2 * padded, :] = row.astype(bf16)
            gs[r + 1, 2 * padded :, :] = behind.astype(bf16)
            return carry

        lax.fori_loop(q * CHUNK, (q + 1) * CHUNK, one, 0)

    def backward(pair):
        rhs = jnp.concatenate(
            [gs[pl.ds(2 * pair + i, 3)].reshape(9 * padded, cols) for i in range(2)], axis=1)
        y = jnp.dot(wb[:, : 9 * padded], rhs, preferred_element_type=f32)
        for i in range(2):
            big[pl.ds(2 * pair + i, channels, stride=rows), :] = y[:, i * cols : (i + 1) * cols]

    g_rows = row_copies(gs, grow_send, grow_recv)
    ready, done = set(), set()

    def runnable():
        new = [p for p in range(1, rows // 2 - 1)
               if p not in done and {2 * p - 1, 2 * p, 2 * p + 1, 2 * p + 2} <= ready]
        done.update(new)
        return new

    for at, q in enumerate(order):
        copies = gradient(q)
        if at == len(order) - 1:
            if len(order) > 2:
                wait_rows(g_rows, gs)
                run_pairs([0], backward)
                run_pairs([rows // 2 - 1], backward)
        for copy in copies:
            copy.wait()
        shifted(q)
        ready.update(range(q * CHUNK, (q + 1) * CHUNK))
        if q == 0:
            start_up(g_rows)
        if q == chunks - 1:
            start_down(g_rows)
        run_pairs(runnable(), backward)
    if len(order) <= 2:
        wait_rows(g_rows, gs)
        run_pairs([0], backward)
        run_pairs([rows // 2 - 1], backward)

    def narrow(c, carry):
        start = pl.multiple_of(c * rows, rows)
        out_ref[c] = big[pl.ds(start, rows), :].astype(bf16)
        return carry

    lax.fori_loop(0, channels, narrow, 0, unroll=4)


def shards(layer_inputs, conv_weight, channel_offset, observed, var_weight):
    _, channels, rows, cols = layer_inputs.shape
    outputs = conv_weight.shape[2]
    members, lats, lons = [lax.axis_size(n) for n in ("member", "lat", "lon")]
    padded = -(-outputs // 16) * 16
    chunks = rows // CHUNK
    sizes = (members, lats, lons, channels, rows, cols, outputs, padded)
    vmem = pl.BlockSpec(memory_space=pltpu.VMEM)
    smem = pl.BlockSpec(memory_space=pltpu.SMEM)
    edge = pltpu.VMEM((chunks, 2, padded, cols), f32)
    dma = pltpu.SemaphoreType.DMA
    predicted, slope = pl.pallas_call(
        functools.partial(kernel, sizes),
        out_shape=(
            jax.ShapeDtypeStruct((outputs, rows, cols), bf16),
            jax.ShapeDtypeStruct((channels, rows, cols), bf16),
        ),
        in_specs=[vmem, vmem, vmem, smem, smem],
        out_specs=(vmem, vmem),
        scratch_shapes=[
            pltpu.VMEM((channels * rows, cols), f32),
            pltpu.VMEM((rows + 2, channels, cols), bf16),
            pltpu.VMEM((3 * padded, 3 * channels), bf16),
            pltpu.VMEM((-(-9 * padded // 128) * 128, channels), bf16),
            pltpu.VMEM((channels, -(-9 * padded // 128) * 128), bf16),
            pltpu.VMEM((padded * rows, cols), f32),
            pltpu.VMEM((padded * rows, cols), f32),
            pltpu.VMEM((rows + 2, 3 * padded, cols), bf16),
            pltpu.VMEM((members - 1, outputs, rows, cols), bf16),
            pltpu.VMEM((rows, cols), f32),
            edge, edge, edge, edge,
            dma((2,)), dma((2,)), dma((2,)), dma((2,)),
            dma((chunks, 2)), dma((chunks, 2)), dma((chunks, 2)), dma((chunks, 2)),
            dma((chunks, members - 1)), dma((chunks, members - 1)),
        ],
        compiler_params=pltpu.CompilerParams(
            collective_id=0, has_side_effects=True, vmem_limit_bytes=60 * 1024 * 1024),
        name="crps_step",
    )(layer_inputs[0], conv_weight, observed, channel_offset, var_weight)
    return predicted[None], slope[None]


def solution(mesh):
    in_specs = (P("member", None, "lat", "lon"), P(), P(), P(None, "lat", "lon"), P())
    out_specs = (P("member", None, "lat", "lon"), P("member", None, "lat", "lon"))
    return jax.shard_map(shards, mesh=mesh, in_specs=in_specs, out_specs=out_specs, check_vma=False)
```

time: 177 us -> 62.6 us (0.35)
  matrix products: 63.7 us -> 0 us
  Pallas kernels: 0 us -> 55.3 us
  waiting for transfers between devices: 38.1 us -> 0 us
  local copies, waits for them, and re-layouts: 33.7 us -> 6.2 us
  starting transfers between devices: 22.7 us -> 0 us
  other arithmetic: 17.6 us -> 0 us
    dot_general x18 -> x0, matrix products: 63.7 us -> none  [the longest x9 52.9 us: shards(): lax.dot_general(conv_weight[row_tap, col_tap], window, (((0,), (0,)), (()...]
    pallas_call x0 -> x1, Pallas kernels: none -> 55.3 us  [shards(): pl.pallas_call(functools.partial(kernel, sizes), out_shape=(jax.ShapeDtyp...]
    all_to_all x2 -> x0, waiting for transfers between devices: 29.5 us -> none  [the longest x1 18.7 us: shards(): lax.all_to_all(pair_block, 'member', split_axis=0, concat_axis=2, tiled=T...]
    ppermute x8 -> x0, starting transfers between devices: 15.1 us -> none  [the longest x4 8.47 us: extended(): before = lax.ppermute(last, axis, up)]
    unnamed x25 -> x2, local copies, waits for them, and re-layouts: 18.8 us -> 6.2 us
    squeeze x2 -> x0, other arithmetic: 9.03 us -> none  [the longest x1 6.6 us: shards(): padded = extend(layer_inputs)[0]]
    ppermute x8 -> x0, waiting for transfers between devices: 8.64 us -> none  [the longest x4 6.57 us: extended(): after = lax.ppermute(initial, axis, down)]
    slice x4 -> x0, local copies, waits for them, and re-layouts: 8.1 us -> none  [the longest x3 7.67 us: extended(): last = lax.slice_in_dim(shard, length - width, length, axis=dim)]
  transfers between devices with their start and end apart: 10 -> 0, of which waited for: 6 -> 0; matrix products, arithmetic and copies ran while one was open for 7% -> 0% of each run, Pallas kernels for 0% -> 0%
where the time goes in v1:
time: 62.6 us; the launch traced here: 62.2 us
  Pallas kernels  55.3 us (88%)
  local copies, waits for them, and re-layouts  6.2 us (10%)
  between operations  0.64 us (1%)
    pallas_call x1, Pallas kernels, shards(): pl.pallas_call(functools.partial(kernel, sizes), out_shape=(jax.ShapeDtyp...  55.3 us
    unnamed x2, local copies, waits for them, and re-layouts  6.2 us

profile of v1, /device:TPU:0, one launch (start us, length us, event | category | flops | bytes accessed | tf_op | source)
XLA Modules:
  0.0 62.2 jit_solution(11250686959539376260)
XLA Ops:
  0.6 55.3 %crps_step.1 = (bf16[69,48,128]{2,1,0:T(8,128)(2,1)}, bf16[256,48,128]{2,1,0:T(8,128)(2,1)}) custom-call(bf16[256,48,128]{2,1,0:T(8,128)(2,1)} %bitcast.3, bf16[3,3,69,256]{3,2,1,0:T(8,128)(2,1)} %w_ref.1, bf16[69,48,128]{2,1,0:T(8,128)(2,1)} %obs_ref.1, f32[69]{0:T(128)} %bias_ref.1, f32[69]{0:T(128)} %var_ref.1), custom_call_target="tpu_custom_call" | custom-call | tf_op jit(solution)/shard_map/crps_step/pallas_call | solution.py:336
  56.0 2.1 %copy.9 = bf16[1,69,48,128]{3,2,1,0:T(8,128)(2,1)} copy(bf16[1,69,48,128]{3,2,1,0:T(8,128)(2,1)} %bitcast.5) | data formatting | bytes 1695744
  58.1 4.1 %copy.10 = bf16[1,256,48,128]{3,2,1,0:T(8,128)(2,1)} copy(bf16[1,256,48,128]{3,2,1,0:T(8,128)(2,1)} %bitcast.4) | data formatting | bytes 6291456

commit v2 on v1

--- a/solution.py
+++ b/solution.py
@@ -15,6 +15,10 @@
 
 def smooth(difference):
     return difference * lax.rsqrt(difference * difference + smoothing * smoothing)
+
+
+def pitch_of(rows):
+    return rows + 8 if rows // 8 % 2 == 0 else rows
 
 
 def kernel(
@@ -27,6 +31,7 @@
     edge_send, edge_recv, gedge_send, gedge_recv, peer_send, peer_recv,
 ):
     members, lats, lons, channels, rows, cols, outputs, padded = sizes
+    pitch = pitch_of(rows)
     chunks = rows // CHUNK
     order = [0] + ([chunks - 1] if chunks > 1 else []) + list(range(1, chunks - 1))
     me, lat, lon = lax.axis_index("member"), lax.axis_index("lat"), lax.axis_index("lon")
@@ -53,14 +58,14 @@
     lax.fori_loop(1, members, greet, 0)
 
     def widen(c, carry):
-        start = pl.multiple_of(c * rows, rows)
+        start = pl.multiple_of(c * pitch, 8)
         big[pl.ds(start, rows), :] = x_ref[c].astype(f32)
         return carry
 
     lax.fori_loop(0, channels, widen, 0, unroll=4)
 
     def turn(r, carry):
-        xt[r + 1] = big[pl.ds(r, channels, stride=rows), :].astype(bf16)
+        xt[r + 1] = big[pl.ds(r, channels, stride=pitch), :].astype(bf16)
         return carry
 
     turn(0, 0)
@@ -127,7 +132,7 @@
             edge_out[q, 1] = jnp.where(lane == r, pltpu.roll(from_right, r + 1, 1), edge_out[q, 1])
             total = mid + jnp.where(lane == 0, 0.0, from_left)
             total = total + jnp.where(lane == cols - 1, 0.0, from_right)
-            pf[pl.ds(r, padded, stride=rows), :] = total
+            pf[pl.ds(r, padded, stride=pitch), :] = total
 
     def edge_copies(q, source, target, send, recv):
         return [
@@ -163,7 +168,7 @@
             copy.wait()
 
         def fix(r, carry):
-            at = pl.ds(r, padded, stride=rows)
+            at = pl.ds(r, padded, stride=pitch)
             left_edge = pltpu.roll(edge_in[q, 0], lax.rem(cols - r, cols), 1)
             right_edge = pltpu.roll(edge_in[q, 1], cols - 1 - r, 1)
             total = pf[at, :]
@@ -174,7 +179,7 @@
         lax.fori_loop(q * CHUNK, (q + 1) * CHUNK, fix, 0)
 
         def pack(o, carry):
-            at = pl.ds(pl.multiple_of(o * rows + q * CHUNK, CHUNK), CHUNK)
+            at = pl.ds(pl.multiple_of(o * pitch + q * CHUNK, 8), CHUNK)
             p_ref[o, q * CHUNK : (q + 1) * CHUNK, :] = (pf[at, :] + bias_ref[o]).astype(bf16)
             return carry
 
@@ -203,8 +208,6 @@
             copy.start()
         if at:
             finish(order[at - 1])
-    finish(order[-1])
-
     wbt[...] = jnp.zeros(wbt.shape, bf16)
     for a in range(3):
         for b in range(3):
@@ -214,14 +217,22 @@
     row_index = (lat * rows + lax.broadcasted_iota(jnp.int32, (rows, cols), 0)).astype(f32)
     latw[...] = jnp.cos((-80.0 + 160.0 * (row_index + 0.5) / float(rows * lats)) * (jnp.pi / 180.0))
 
-    def misfit(o, carry):
-        at = pl.ds(pl.multiple_of(o * rows, rows), rows)
-        g[at, :] = smooth(p_ref[o].astype(f32) - obs_ref[o].astype(f32))
-        return carry
-
-    lax.fori_loop(0, outputs, misfit, 0, unroll=3)
-    g[pl.ds(outputs * rows, (padded - outputs) * rows), :] = jnp.zeros(
-        ((padded - outputs) * rows, cols), f32)
+    def misfits(q):
+        inside = slice(q * CHUNK, (q + 1) * CHUNK)
+
+        def misfit(o, carry):
+            at = pl.ds(pl.multiple_of(o * pitch + q * CHUNK, 8), CHUNK)
+            g[at, :] = smooth(p_ref[o, inside, :].astype(f32) - obs_ref[o, inside, :].astype(f32))
+            return carry
+
+        lax.fori_loop(0, outputs, misfit, 0, unroll=3)
+
+    g[pl.ds(outputs * pitch, (padded - outputs) * pitch), :] = jnp.zeros(
+        ((padded - outputs) * pitch, cols), f32)
+    for q in order[:-1]:
+        misfits(q)
+    finish(order[-1])
+    misfits(order[-1])
 
     def gradient(q):
         inside = slice(q * CHUNK, (q + 1) * CHUNK)
@@ -234,7 +245,7 @@
         weight_row = latw[inside, :]
 
         def score(o, carry):
-            at = pl.ds(pl.multiple_of(o * rows + q * CHUNK, CHUNK), CHUNK)
+            at = pl.ds(pl.multiple_of(o * pitch + q * CHUNK, 8), CHUNK)
             own = p_ref[o, inside, :].astype(f32)
             add = lambda j, run: run + smooth(own - others[j, o, inside, :].astype(f32))
             pair_sum = smooth(own - own)
@@ -250,7 +261,7 @@
 
         def collect(r, carry):
             to_right, to_left = carry
-            row = g[pl.ds(r, padded, stride=rows), :]
+            row = g[pl.ds(r, padded, stride=pitch), :]
             to_right = jnp.where(lane == r, pltpu.roll(row, r + 1, 1), to_right)
             to_left = jnp.where(lane == r, pltpu.roll(row, r, 1), to_left)
             return to_right, to_left
@@ -265,7 +276,7 @@
 
     def shifted(q):
         def one(r, carry):
-            row = g[pl.ds(r, padded, stride=rows), :]
+            row = g[pl.ds(r, padded, stride=pitch), :]
             left_edge = pltpu.roll(gedge_in[q, 0], lax.rem(cols - r, cols), 1)
             right_edge = pltpu.roll(gedge_in[q, 1], cols - 1 - r, 1)
             ahead = jnp.where(lane == cols - 1, right_edge, pltpu.roll(row, cols - 1, 1))
@@ -282,7 +293,7 @@
             [gs[pl.ds(2 * pair + i, 3)].reshape(9 * padded, cols) for i in range(2)], axis=1)
         y = jnp.dot(wb[:, : 9 * padded], rhs, preferred_element_type=f32)
         for i in range(2):
-            big[pl.ds(2 * pair + i, channels, stride=rows), :] = y[:, i * cols : (i + 1) * cols]
+            big[pl.ds(2 * pair + i, channels, stride=pitch), :] = y[:, i * cols : (i + 1) * cols]
 
     g_rows = row_copies(gs, grow_send, grow_recv)
     ready, done = set(), set()
@@ -293,13 +304,7 @@
         done.update(new)
         return new
 
-    for at, q in enumerate(order):
-        copies = gradient(q)
-        if at == len(order) - 1:
-            if len(order) > 2:
-                wait_rows(g_rows, gs)
-                run_pairs([0], backward)
-                run_pairs([rows // 2 - 1], backward)
+    def settle(q, copies):
         for copy in copies:
             copy.wait()
         shifted(q)
@@ -308,14 +313,29 @@
             start_up(g_rows)
         if q == chunks - 1:
             start_down(g_rows)
-        run_pairs(runnable(), backward)
+
+    early = order[:-1]
+    moving = [(q, gradient(q)) for q in early]
+    for q, copies in moving:
+        settle(q, copies)
+    work = runnable()
+    run_pairs(work[: len(work) // 2], backward)
+    last = order[-1]
+    copies = gradient(last)
+    run_pairs(work[len(work) // 2 :], backward)
+    if len(order) > 2:
+        wait_rows(g_rows, gs)
+        run_pairs([0], backward)
+        run_pairs([rows // 2 - 1], backward)
+    settle(last, copies)
+    run_pairs(runnable(), backward)
     if len(order) <= 2:
         wait_rows(g_rows, gs)
         run_pairs([0], backward)
         run_pairs([rows // 2 - 1], backward)
 
     def narrow(c, carry):
-        start = pl.multiple_of(c * rows, rows)
+        start = pl.multiple_of(c * pitch, 8)
         out_ref[c] = big[pl.ds(start, rows), :].astype(bf16)
         return carry
 
@@ -336,19 +356,19 @@
     predicted, slope = pl.pallas_call(
         functools.partial(kernel, sizes),
         out_shape=(
-            jax.ShapeDtypeStruct((outputs, rows, cols), bf16),
-            jax.ShapeDtypeStruct((channels, rows, cols), bf16),
+            pltpu.VMEM((outputs, rows, cols), bf16),
+            pltpu.VMEM((channels, rows, cols), bf16),
         ),
         in_specs=[vmem, vmem, vmem, smem, smem],
         out_specs=(vmem, vmem),
         scratch_shapes=[
-            pltpu.VMEM((channels * rows, cols), f32),
+            pltpu.VMEM((channels * pitch_of(rows), cols), f32),
             pltpu.VMEM((rows + 2, channels, cols), bf16),
             pltpu.VMEM((3 * padded, 3 * channels), bf16),
             pltpu.VMEM((-(-9 * padded // 128) * 128, channels), bf16),
             pltpu.VMEM((channels, -(-9 * padded // 128) * 128), bf16),
-            pltpu.VMEM((padded * rows, cols), f32),
-            pltpu.VMEM((padded * rows, cols), f32),
+            pltpu.VMEM((padded * pitch_of(rows), cols), f32),
+            pltpu.VMEM((padded * pitch_of(rows), cols), f32),
             pltpu.VMEM((rows + 2, 3 * padded, cols), bf16),
             pltpu.VMEM((members - 1, outputs, rows, cols), bf16),
             pltpu.VMEM((rows, cols), f32),

time: 62.6 us -> 51.7 us (0.83)
  Pallas kernels: 55.3 us -> 48.4 us
  local copies, waits for them, and re-layouts: 6.2 us -> 2.57 us
    pallas_call x1, Pallas kernels: 55.3 us -> 48.4 us  [shards(): pl.pallas_call(functools.partial(kernel, sizes), out_shape=(pltpu.VMEM((o...]
    unnamed x2, local copies, waits for them, and re-layouts: 6.2 us -> 2.57 us
where the time goes in v2:
time: 51.7 us; the launch traced here: 51.6 us
  Pallas kernels  48.4 us (94%)
  local copies, waits for them, and re-layouts  2.57 us (5%)
  between operations  0.64 us (1%)
    pallas_call x1, Pallas kernels, shards(): pl.pallas_call(functools.partial(kernel, sizes), out_shape=(pltpu.VMEM((o...  48.4 us
    unnamed x2, local copies, waits for them, and re-layouts  2.57 us

profile of v2, /device:TPU:0, one launch (start us, length us, event | category | flops | bytes accessed | tf_op | source)
XLA Modules:
  0.0 51.6 jit_solution(1820465740440994298)
XLA Ops:
  0.6 48.4 %crps_step.1 = (bf16[69,48,128]{2,1,0:T(8,128)(2,1)S(1)}, bf16[256,48,128]{2,1,0:T(8,128)(2,1)S(1)}) custom-call(bf16[256,48,128]{2,1,0:T(8,128)(2,1)} %bitcast.5, bf16[3,3,69,256]{3,2,1,0:T(8,128)(2,1)} %w_ref.1, bf16[69,48,128]{2,1,0:T(8,128)(2,1)} %obs_ref.1, f32[69]{0:T(128)} %bias_ref.1, f32[69]{0:T(128)} %var_ref.1), custom_call_target="tpu_custom_call" | custom-call | tf_op jit(solution)/shard_map/crps_step/pallas_call | solution.py:356
  49.0 0.9 %copy.9 = bf16[1,69,48,128]{3,2,1,0:T(8,128)(2,1)} copy(bf16[1,69,48,128]{3,2,1,0:T(8,128)(2,1)S(1)} %bitcast.4) | data formatting | bytes 1695744
  49.9 1.7 %copy.10 = bf16[1,256,48,128]{3,2,1,0:T(8,128)(2,1)} copy(bf16[1,256,48,128]{3,2,1,0:T(8,128)(2,1)S(1)} %bitcast.3) | data formatting | bytes 6291456

commit v3 on v2

--- a/solution.py
+++ b/solution.py
@@ -1,4 +1,5 @@
 import functools
+import math
 
 import jax
 import jax.numpy as jnp
@@ -23,21 +24,32 @@
 
 def kernel(
     sizes,
-    x_ref, w_ref, obs_ref, bias_ref, var_ref,
+    x_hbm, w_hbm, obs_hbm, bias_ref, var_ref,
     p_ref, out_ref,
-    big, xt, wf, wbt, wb, pf, g, gs, others, latw,
-    edge_out, edge_in, gedge_out, gedge_in,
+    x_ref, w_ref, obs_ref, load_sem, big, xt, wf, wbt, wb, pf, g, gs, others, latw,
+    turned, edge_out, edge_in, gedge_out, gedge_in,
     row_send, row_recv, grow_send, grow_recv,
     edge_send, edge_recv, gedge_send, gedge_recv, peer_send, peer_recv,
 ):
     members, lats, lons, channels, rows, cols, outputs, padded = sizes
     pitch = pitch_of(rows)
+    spread = max(d for d in range(1, 25) if outputs % d == 0)
     chunks = rows // CHUNK
     order = [0] + ([chunks - 1] if chunks > 1 else []) + list(range(1, chunks - 1))
     me, lat, lon = lax.axis_index("member"), lax.axis_index("lat"), lax.axis_index("lon")
     right, left = lax.rem(lon + 1, lons), lax.rem(lon + lons - 1, lons)
     has_up, has_down = lat > 0, lat < lats - 1
 
+    loads = {
+        q: pltpu.make_async_copy(
+            x_hbm.at[:, pl.ds(q * CHUNK, CHUNK), :], x_ref.at[:, pl.ds(q * CHUNK, CHUNK), :],
+            load_sem.at[q])
+        for q in order}
+    loads["w"] = pltpu.make_async_copy(w_hbm, w_ref, load_sem.at[chunks])
+    loads["obs"] = pltpu.make_async_copy(obs_hbm, obs_ref, load_sem.at[chunks + 1])
+    for load in loads.values():
+        load.start()
+
     barrier = pltpu.get_barrier_semaphore()
     for side in (left, right):
         pl.semaphore_signal(barrier, inc=1, device_id=(me, lat, side), device_id_type=MESH)
@@ -57,17 +69,22 @@
 
     lax.fori_loop(1, members, greet, 0)
 
-    def widen(c, carry):
-        start = pl.multiple_of(c * pitch, 8)
-        big[pl.ds(start, rows), :] = x_ref[c].astype(f32)
-        return carry
-
-    lax.fori_loop(0, channels, widen, 0, unroll=4)
+    def widen(q):
+        loads[q].wait()
+
+        def one(c, carry):
+            at = pl.ds(pl.multiple_of(c * pitch + q * CHUNK, 8), CHUNK)
+            big[at, :] = x_ref[c, q * CHUNK : (q + 1) * CHUNK, :].astype(f32)
+            return carry
+
+        lax.fori_loop(0, channels, one, 0, unroll=16)
 
     def turn(r, carry):
         xt[r + 1] = big[pl.ds(r, channels, stride=pitch), :].astype(bf16)
         return carry
 
+    for q in order[:2]:
+        widen(q)
     turn(0, 0)
     turn(rows - 1, 0)
     pl.semaphore_wait(barrier, members + 1 + has_up.astype(jnp.int32) + has_down.astype(jnp.int32))
@@ -109,7 +126,13 @@
     x_rows = row_copies(xt, row_send, row_recv)
     start_up(x_rows)
     start_down(x_rows)
-    lax.fori_loop(1, rows - 1, turn, 0)
+    lax.fori_loop(1, CHUNK, turn, 0, unroll=3)
+    if chunks > 1:
+        lax.fori_loop(rows - CHUNK, rows - 1, turn, 0, unroll=3)
+    for q in order[2:]:
+        widen(q)
+        lax.fori_loop(q * CHUNK, (q + 1) * CHUNK, turn, 0, unroll=2)
+    loads["w"].wait()
 
     wf[...] = jnp.zeros(wf.shape, bf16)
     for a in range(3):
@@ -117,6 +140,7 @@
             wf[b * padded : b * padded + outputs, a * channels : (a + 1) * channels] = w_ref[a, b]
 
     lane = lax.broadcasted_iota(jnp.int32, (padded, cols), 1)
+    thin = lax.broadcasted_iota(jnp.int32, (CHUNK, cols), 1)
 
     def forward(pair, q):
         rhs = jnp.concatenate(
@@ -128,8 +152,9 @@
                 y[b * padded : (b + 1) * padded, i * cols : (i + 1) * cols] for b in range(3)]
             from_left = pltpu.roll(from_left, 1, 1)
             from_right = pltpu.roll(from_right, cols - 1, 1)
-            edge_out[q, 0] = jnp.where(lane == r, pltpu.roll(from_left, r, 1), edge_out[q, 0])
-            edge_out[q, 1] = jnp.where(lane == r, pltpu.roll(from_right, r + 1, 1), edge_out[q, 1])
+            slot = r - q * CHUNK
+            both = pltpu.roll(jnp.where(lane == 0, from_left, from_right), 2 * slot + 1, 1)
+            turned[0, 0:padded, :] = jnp.where(lane // 2 == slot, both, turned[0, 0:padded, :])
             total = mid + jnp.where(lane == 0, 0.0, from_left)
             total = total + jnp.where(lane == cols - 1, 0.0, from_right)
             pf[pl.ds(r, padded, stride=pitch), :] = total
@@ -152,7 +177,7 @@
                 body(pair)
                 return carry
 
-            lax.fori_loop(pairs[0], pairs[0] + n, step, 0)
+            lax.fori_loop(pairs[0], pairs[0] + n, step, 0, unroll=math.gcd(n, 2) if n % 2 == 0 else n if n < 8 else 1)
             pairs = pairs[n:]
 
     peer = lambda q, step: pltpu.make_async_remote_copy(
@@ -167,23 +192,17 @@
         for copy in edges[q]:
             copy.wait()
 
-        def fix(r, carry):
-            at = pl.ds(r, padded, stride=pitch)
-            left_edge = pltpu.roll(edge_in[q, 0], lax.rem(cols - r, cols), 1)
-            right_edge = pltpu.roll(edge_in[q, 1], cols - 1 - r, 1)
-            total = pf[at, :]
-            total = total + jnp.where(lane == 0, left_edge, 0.0)
-            pf[at, :] = total + jnp.where(lane == cols - 1, right_edge, 0.0)
-            return carry
-
-        lax.fori_loop(q * CHUNK, (q + 1) * CHUNK, fix, 0)
+        left_edge, right_edge = edge_in[q, 0], edge_in[q, 1]
 
         def pack(o, carry):
             at = pl.ds(pl.multiple_of(o * pitch + q * CHUNK, 8), CHUNK)
-            p_ref[o, q * CHUNK : (q + 1) * CHUNK, :] = (pf[at, :] + bias_ref[o]).astype(bf16)
-            return carry
-
-        lax.fori_loop(0, outputs, pack, 0, unroll=3)
+            total = pf[at, :]
+            total = total + jnp.where(thin == 0, pltpu.roll(left_edge, lax.rem(cols - o, cols), 1), 0.0)
+            total = total + jnp.where(thin == cols - 1, pltpu.roll(right_edge, cols - 1 - o, 1), 0.0)
+            p_ref[o, q * CHUNK : (q + 1) * CHUNK, :] = (total + bias_ref[o]).astype(bf16)
+            return carry
+
+        lax.fori_loop(0, outputs, pack, 0, unroll=spread)
 
         def send(step, carry):
             peer(q, step).start()
@@ -192,9 +211,9 @@
         lax.fori_loop(1, members, send, 0)
 
     half = CHUNK // 2
+    turned[0] = jnp.zeros(turned.shape[1:], f32)
     waited = False
     for at, q in enumerate(order):
-        edge_out[q] = jnp.zeros(edge_out.shape[1:], f32)
         pairs = range(q * half, (q + 1) * half)
         bounds = [p for p in pairs if p in (0, rows // 2 - 1)]
         run_pairs([p for p in pairs if p not in bounds], lambda p: forward(p, q))
@@ -203,6 +222,9 @@
             waited = True
         for p in bounds:
             forward(p, q)
+        turned[1] = jnp.transpose(turned[0])
+        edge_out[q, 0] = turned[1, pl.ds(1, CHUNK, stride=2), :]
+        edge_out[q, 1] = turned[1, pl.ds(0, CHUNK, stride=2), :]
         edges[q] = edge_copies(q, edge_out, edge_in, edge_send, edge_recv)
         for copy in edges[q]:
             copy.start()
@@ -217,6 +239,8 @@
     row_index = (lat * rows + lax.broadcasted_iota(jnp.int32, (rows, cols), 0)).astype(f32)
     latw[...] = jnp.cos((-80.0 + 160.0 * (row_index + 0.5) / float(rows * lats)) * (jnp.pi / 180.0))
 
+    loads["obs"].wait()
+
     def misfits(q):
         inside = slice(q * CHUNK, (q + 1) * CHUNK)
 
@@ -225,7 +249,7 @@
             g[at, :] = smooth(p_ref[o, inside, :].astype(f32) - obs_ref[o, inside, :].astype(f32))
             return carry
 
-        lax.fori_loop(0, outputs, misfit, 0, unroll=3)
+        lax.fori_loop(0, outputs, misfit, 0, unroll=spread)
 
     g[pl.ds(outputs * pitch, (padded - outputs) * pitch), :] = jnp.zeros(
         ((padded - outputs) * pitch, cols), f32)
@@ -254,39 +278,37 @@
             else:
                 pair_sum = lax.fori_loop(0, members - 1, add, pair_sum)
             value = weight_row * var_ref[o] * (g[at, :] - pair_sum / (members - 1))
-            g[at, :] = value.astype(bf16).astype(f32)
-            return carry
-
-        lax.fori_loop(0, outputs, score, 0, unroll=3)
-
-        def collect(r, carry):
+            value = value.astype(bf16).astype(f32)
+            g[at, :] = value
             to_right, to_left = carry
-            row = g[pl.ds(r, padded, stride=pitch), :]
-            to_right = jnp.where(lane == r, pltpu.roll(row, r + 1, 1), to_right)
-            to_left = jnp.where(lane == r, pltpu.roll(row, r, 1), to_left)
+            to_right = jnp.where(thin == o, pltpu.roll(value, o + 1, 1), to_right)
+            to_left = jnp.where(thin == o, pltpu.roll(value, o, 1), to_left)
             return to_right, to_left
 
-        zero = jnp.zeros((padded, cols), f32)
+        zero = jnp.zeros((CHUNK, cols), f32)
         gedge_out[q, 0], gedge_out[q, 1] = lax.fori_loop(
-            q * CHUNK, (q + 1) * CHUNK, collect, (zero, zero))
+            0, outputs, score, (zero, zero), unroll=spread)
         copies = edge_copies(q, gedge_out, gedge_in, gedge_send, gedge_recv)
         for copy in copies:
             copy.start()
         return copies
 
     def shifted(q):
+        turned[1, pl.ds(0, CHUNK, stride=2), :] = gedge_in[q, 1]
+        turned[1, pl.ds(1, CHUNK, stride=2), :] = gedge_in[q, 0]
+        turned[0] = jnp.transpose(turned[1])
+
         def one(r, carry):
             row = g[pl.ds(r, padded, stride=pitch), :]
-            left_edge = pltpu.roll(gedge_in[q, 0], lax.rem(cols - r, cols), 1)
-            right_edge = pltpu.roll(gedge_in[q, 1], cols - 1 - r, 1)
-            ahead = jnp.where(lane == cols - 1, right_edge, pltpu.roll(row, cols - 1, 1))
-            behind = jnp.where(lane == 0, left_edge, pltpu.roll(row, 1, 1))
+            both = pltpu.roll(turned[0, 0:padded, :], cols - 1 - 2 * (r - q * CHUNK), 1)
+            ahead = jnp.where(lane == cols - 1, both, pltpu.roll(row, cols - 1, 1))
+            behind = jnp.where(lane == 0, both, pltpu.roll(row, 1, 1))
             gs[r + 1, 0:padded, :] = ahead.astype(bf16)
             gs[r + 1, padded : 2 * padded, :] = row.astype(bf16)
             gs[r + 1, 2 * padded :, :] = behind.astype(bf16)
             return carry
 
-        lax.fori_loop(q * CHUNK, (q + 1) * CHUNK, one, 0)
+        lax.fori_loop(q * CHUNK, (q + 1) * CHUNK, one, 0, unroll=4)
 
     def backward(pair):
         rhs = jnp.concatenate(
@@ -339,7 +361,7 @@
         out_ref[c] = big[pl.ds(start, rows), :].astype(bf16)
         return carry
 
-    lax.fori_loop(0, channels, narrow, 0, unroll=4)
+    lax.fori_loop(0, channels, narrow, 0, unroll=8)
 
 
 def shards(layer_inputs, conv_weight, channel_offset, observed, var_weight):
@@ -351,7 +373,8 @@
     sizes = (members, lats, lons, channels, rows, cols, outputs, padded)
     vmem = pl.BlockSpec(memory_space=pltpu.VMEM)
     smem = pl.BlockSpec(memory_space=pltpu.SMEM)
-    edge = pltpu.VMEM((chunks, 2, padded, cols), f32)
+    edge = pltpu.VMEM((chunks, 2, CHUNK, cols), f32)
+    hbm = pl.BlockSpec(memory_space=pl.ANY)
     dma = pltpu.SemaphoreType.DMA
     predicted, slope = pl.pallas_call(
         functools.partial(kernel, sizes),
@@ -359,9 +382,13 @@
             pltpu.VMEM((outputs, rows, cols), bf16),
             pltpu.VMEM((channels, rows, cols), bf16),
         ),
-        in_specs=[vmem, vmem, vmem, smem, smem],
+        in_specs=[hbm, hbm, hbm, smem, smem],
         out_specs=(vmem, vmem),
         scratch_shapes=[
+            pltpu.VMEM((channels, rows, cols), bf16),
+            pltpu.VMEM(conv_weight.shape, bf16),
+            pltpu.VMEM((outputs, rows, cols), bf16),
+            dma((chunks + 2,)),
             pltpu.VMEM((channels * pitch_of(rows), cols), f32),
             pltpu.VMEM((rows + 2, channels, cols), bf16),
             pltpu.VMEM((3 * padded, 3 * channels), bf16),
@@ -372,6 +399,7 @@
             pltpu.VMEM((rows + 2, 3 * padded, cols), bf16),
             pltpu.VMEM((members - 1, outputs, rows, cols), bf16),
             pltpu.VMEM((rows, cols), f32),
+            pltpu.VMEM((2, cols, cols), f32),
             edge, edge, edge, edge,
             dma((2,)), dma((2,)), dma((2,)), dma((2,)),
             dma((chunks, 2)), dma((chunks, 2)), dma((chunks, 2)), dma((chunks, 2)),

time: 51.7 us -> 41.2 us (0.80)
  Pallas kernels: 48.4 us -> 37.9 us
    pallas_call x1, Pallas kernels: 48.4 us -> 37.9 us  [shards(): pl.pallas_call(functools.partial(kernel, sizes), out_shape=(pltpu.VMEM((o...]
where the time goes in v3:
time: 41.2 us; the launch traced here: 41.1 us
  Pallas kernels  37.9 us (92%)
  local copies, waits for them, and re-layouts  2.57 us (6%)
  between operations  0.64 us (2%)
    pallas_call x1, Pallas kernels, shards(): pl.pallas_call(functools.partial(kernel, sizes), out_shape=(pltpu.VMEM((o...  37.9 us
    unnamed x2, local copies, waits for them, and re-layouts  2.57 us

profile of v3, /device:TPU:0, one launch (start us, length us, event | category | flops | bytes accessed | tf_op | source)
XLA Modules:
  0.0 41.1 jit_solution(7532976466591132078)
XLA Ops:
  0.6 37.9 %crps_step.1 = (bf16[69,48,128]{2,1,0:T(8,128)(2,1)S(1)}, bf16[256,48,128]{2,1,0:T(8,128)(2,1)S(1)}) custom-call(bf16[256,48,128]{2,1,0:T(8,128)(2,1)} %bitcast.5, bf16[3,3,69,256]{3,2,1,0:T(8,128)(2,1)} %w_hbm.1, bf16[69,48,128]{2,1,0:T(8,128)(2,1)} %obs_hbm.1, f32[69]{0:T(128)} %bias_ref.1, f32[69]{0:T(128)} %var_ref.1), custom_call_target="tpu_custom_call" | custom-call | tf_op jit(solution)/shard_map/crps_step/pallas_call | solution.py:379
  38.5 0.9 %copy.9 = bf16[1,69,48,128]{3,2,1,0:T(8,128)(2,1)} copy(bf16[1,69,48,128]{3,2,1,0:T(8,128)(2,1)S(1)} %bitcast.4) | data formatting | bytes 1695744
  39.4 1.7 %copy.10 = bf16[1,256,48,128]{3,2,1,0:T(8,128)(2,1)} copy(bf16[1,256,48,128]{3,2,1,0:T(8,128)(2,1)S(1)} %bitcast.3) | data formatting | bytes 6291456

commit v4 on v3

--- a/solution.py
+++ b/solution.py
@@ -127,11 +127,15 @@
     start_up(x_rows)
     start_down(x_rows)
     lax.fori_loop(1, CHUNK, turn, 0, unroll=3)
-    if chunks > 1:
-        lax.fori_loop(rows - CHUNK, rows - 1, turn, 0, unroll=3)
     for q in order[2:]:
         widen(q)
-        lax.fori_loop(q * CHUNK, (q + 1) * CHUNK, turn, 0, unroll=2)
+    if chunks > 1:
+        turn(CHUNK, 0)
+
+    def turn_rest():
+        if chunks > 1:
+            lax.fori_loop(CHUNK + 1, rows - 1, turn, 0, unroll=2)
+
     loads["w"].wait()
 
     wf[...] = jnp.zeros(wf.shape, bf16)
@@ -228,7 +232,11 @@
         edges[q] = edge_copies(q, edge_out, edge_in, edge_send, edge_recv)
         for copy in edges[q]:
             copy.start()
-        if at:
+        if at == 0:
+            turn_rest()
+        if at == 0 and len(order) > 1:
+            finish(q)
+        elif at > 1:
             finish(order[at - 1])
     wbt[...] = jnp.zeros(wbt.shape, bf16)
     for a in range(3):

time: 41.2 us -> 41.2 us (level)
  no operation moved by 1% of the time
where the time goes in v4:
time: 41.2 us; the launch traced here: 41.1 us
  Pallas kernels  37.9 us (92%)
  local copies, waits for them, and re-layouts  2.57 us (6%)
  between operations  0.64 us (2%)
    pallas_call x1, Pallas kernels, shards(): pl.pallas_call(functools.partial(kernel, sizes), out_shape=(pltpu.VMEM((o...  37.9 us
    unnamed x2, local copies, waits for them, and re-layouts  2.57 us

profile of v4, /device:TPU:0, one launch (start us, length us, event | category | flops | bytes accessed | tf_op | source)
XLA Modules:
  0.0 41.1 jit_solution(11398364030422190637)
XLA Ops:
  0.6 37.9 %crps_step.1 = (bf16[69,48,128]{2,1,0:T(8,128)(2,1)S(1)}, bf16[256,48,128]{2,1,0:T(8,128)(2,1)S(1)}) custom-call(bf16[256,48,128]{2,1,0:T(8,128)(2,1)} %bitcast.5, bf16[3,3,69,256]{3,2,1,0:T(8,128)(2,1)} %w_hbm.1, bf16[69,48,128]{2,1,0:T(8,128)(2,1)} %obs_hbm.1, f32[69]{0:T(128)} %bias_ref.1, f32[69]{0:T(128)} %var_ref.1), custom_call_target="tpu_custom_call" | custom-call | tf_op jit(solution)/shard_map/crps_step/pallas_call | solution.py:387
  38.5 0.9 %copy.9 = bf16[1,69,48,128]{3,2,1,0:T(8,128)(2,1)} copy(bf16[1,69,48,128]{3,2,1,0:T(8,128)(2,1)S(1)} %bitcast.4) | data formatting | bytes 1695744
  39.4 1.7 %copy.10 = bf16[1,256,48,128]{3,2,1,0:T(8,128)(2,1)} copy(bf16[1,256,48,128]{3,2,1,0:T(8,128)(2,1)S(1)} %bitcast.3) | data formatting | bytes 6291456
